TPU v7x, 32 devices: a whole 2x2x4 slice. The times are simulated.
32 devices in a mesh: dp: 4 (over y, core), fsdp: 8 (over z, x).
Axes of the slice: x: 2, y: 2, z: 4, core: 2. Of those that a mesh axis runs over, the one named last changes fastest.
Arguments:
- data_samples: bfloat16 [512, 4096], P('dp', 'fsdp'), may hold values from -6 to 6
- negative_start: float32 [512, 4096], P('dp', 'fsdp'), may hold values from -6 to 6
- langevin_noise: float32 [4, 512, 4096], P(None, 'dp', 'fsdp'), may hold values from -6 to 6
- first_weight: bfloat16 [4096, 4096], P('fsdp'), may hold values from -0.09375 to 0.09375
- second_weight: bfloat16 [4096, 4096], P('fsdp'), may hold values from -0.09375 to 0.09375
- readout: float32 [4096], P('fsdp'), may hold values from -480 to 480
Outputs:
- first_grad: float32 [4096, 4096], P('fsdp', 'dp')
- second_grad: float32 [4096, 4096], P('fsdp', 'dp')
- energy_gap: float32 [], replicated
All inputs are finite; a program needn't handle non-finite values.
Results may differ from a plain program's by a relative error of at most 0.014.
Values may be sent and summed in bfloat16 or wider, within the bound.
A program may use at most 64 MiB of HBM per device.

v0:
```python
import jax
import jax.numpy as jnp
from jax import lax
from jax.sharding import PartitionSpec as P

D = 4096
H = 4096
STEPS = 4


def slope(values):
    sig = jax.nn.sigmoid(values)
    return sig * (1.0 + values * (1.0 - sig))


def forward(inputs, first_weight, second_weight):
    term_one = jnp.dot(inputs, first_weight, preferred_element_type=jnp.float32)
    pre_one = lax.psum_scatter(
        term_one.astype(jnp.bfloat16), "fsdp", scatter_dimension=1, tiled=True
    ).astype(jnp.float32)
    hidden = jax.nn.silu(pre_one).astype(jnp.bfloat16)
    term_two = jnp.dot(hidden, second_weight, preferred_element_type=jnp.float32)
    pre_two = lax.psum_scatter(
        term_two.astype(jnp.bfloat16), "fsdp", scatter_dimension=1, tiled=True
    ).astype(jnp.float32)
    return (pre_one, hidden, pre_two)


def backward(cotan, readout, pre_one, pre_two, second_weight):
    grad_two = (cotan[:, None] * readout[None, :] * slope(pre_two)).astype(jnp.bfloat16)
    full_two = lax.all_gather(grad_two, "fsdp", axis=1, tiled=True)
    back_one = lax.dot_general(
        full_two, second_weight, (((1,), (1,)), ((), ())), preferred_element_type=jnp.float32
    )
    grad_one = (back_one * slope(pre_one)).astype(jnp.bfloat16)
    full_one = lax.all_gather(grad_one, "fsdp", axis=1, tiled=True)
    return (full_two, full_one)


def contract_rows(left, right):
    return lax.dot_general(
        left, right, (((0,), (0,)), ((), ())), preferred_element_type=jnp.float32
    )


def one_pass(inputs, cotan, readout, first_weight, second_weight):
    pre_one, hidden, pre_two = forward(inputs, first_weight, second_weight)
    energies = jnp.dot(jax.nn.silu(pre_two), readout, precision=lax.Precision.HIGHEST)
    full_two, full_one = backward(cotan, readout, pre_one, pre_two, second_weight)
    raw_one = contract_rows(inputs, full_one)
    raw_two = contract_rows(hidden, full_two)
    return (jnp.sum(cotan * energies), raw_one, raw_two)


def local(data_samples, negative_start, langevin_noise, first_weight, second_weight, readout):
    state = negative_start
    ones = jnp.ones((state.shape[0],), jnp.float32)
    for step in range(STEPS):
        inputs = state.astype(jnp.bfloat16)
        pre_one, hidden, pre_two = forward(inputs, first_weight, second_weight)
        full_two, full_one = backward(ones, readout, pre_one, pre_two, second_weight)
        moved = lax.dot_general(
            full_one, first_weight, (((1,), (1,)), ((), ())), preferred_element_type=jnp.float32
        )
        state = state - 0.005 * moved + 0.1 * langevin_noise[step]
    negatives = state.astype(jnp.bfloat16)
    rows = jnp.concatenate([data_samples, negatives], axis=0)
    cotan = jnp.concatenate([ones, -ones])
    signed, raw_one, raw_two = one_pass(rows, cotan, readout, first_weight, second_weight)
    group_one, group_two = (
        lax.psum_scatter(raw_one, "dp", scatter_dimension=1, tiled=True),
        lax.psum_scatter(raw_two, "dp", scatter_dimension=1, tiled=True),
    )
    squares = jnp.sum(group_one * group_one) + jnp.sum(group_two * group_two)
    signed_total = lax.psum(signed, ("dp", "fsdp"))
    square_total = lax.psum(squares, ("dp", "fsdp"))
    energy_gap = signed_total / (
        state.shape[0] * lax.axis_size("dp") * 80.0 * jnp.sqrt(jnp.float32(H))
    )
    scale = jnp.sqrt(square_total / (2.0 * D * H) + 1e-06)
    return (group_one / scale, group_two / scale, energy_gap)


def solution(mesh):
    in_specs = (
        P("dp", "fsdp"),
        P("dp", "fsdp"),
        P(None, "dp", "fsdp"),
        P("fsdp", None),
        P("fsdp", None),
        P("fsdp"),
    )
    out_specs = (P("fsdp", "dp"), P("fsdp", "dp"), P())
    return jax.shard_map(local, mesh=mesh, in_specs=in_specs, out_specs=out_specs, check_vma=False)
```

profile of v0, /device:TPU:0, one launch (start us, length us, event | category | flops | bytes accessed | tf_op | source)
XLA Modules:
  0.0 1354.0 jit_solution(11661609646808757487)
XLA Ops:
  11.3 68.2 %reduce-scatter.13.cloned.1.call-done = bf16[128,512]{1,0:T(8,128)(2,1)} async-done(((bf16[128,4096]{1,0:T(8,128)(2,1)}), bf16[128,512]{1,0:T(8,128)(2,1)}) %reduce-scatter.13.cloned.1.call-update) | async-done | bytes 131088 | tf_op jit(solution)/shard_map/reduce_scatter | solution.py:18
  83.5 63.7 %reduce-scatter.15.cloned.1.call-done = bf16[128,512]{1,0:T(8,128)(2,1)} async-done(((bf16[128,4096]{1,0:T(8,128)(2,1)}), bf16[128,512]{1,0:T(8,128)(2,1)}) %reduce-scatter.15.cloned.1.call-update) | async-done | bytes 131088 | tf_op jit(solution)/shard_map/reduce_scatter | solution.py:23
  149.0 39.2 %all-gather.11.cloned.1.call-done = bf16[128,4096]{1,0:T(8,128)(2,1)} async-done(((bf16[128,512]{1,0:T(8,128)(2,1)}), bf16[128,4096]{1,0:T(8,128)(2,1)}) %all-gather.11.cloned.1.call-update) | async-done | bytes 1048592 | tf_op jit(solution)/shard_map/all_gather | solution.py:31
  188.2 4.7 fusion.9
  193.0 38.5 %all-gather.13.cloned.1.call-done = bf16[128,4096]{1,0:T(8,128)(2,1)} async-done(((bf16[128,512]{1,0:T(8,128)(2,1)}), bf16[128,4096]{1,0:T(8,128)(2,1)}) %all-gather.13.cloned.1.call-update) | async-done | bytes 1048592 | tf_op jit(solution)/shard_map/all_gather | solution.py:36
  237.5 63.8 %reduce-scatter.17.cloned.1.call-done = bf16[128,512]{1,0:T(8,128)(2,1)} async-done(((bf16[128,4096]{1,0:T(8,128)(2,1)}), bf16[128,512]{1,0:T(8,128)(2,1)}) %reduce-scatter.17.cloned.1.call-update) | async-done | bytes 131088 | tf_op jit(solution)/shard_map/reduce_scatter | solution.py:18
  305.4 63.8 %reduce-scatter.19.cloned.1.call-done = bf16[128,512]{1,0:T(8,128)(2,1)} async-done(((bf16[128,4096]{1,0:T(8,128)(2,1)}), bf16[128,512]{1,0:T(8,128)(2,1)}) %reduce-scatter.19.cloned.1.call-update) | async-done | bytes 131088 | tf_op jit(solution)/shard_map/reduce_scatter | solution.py:23
  370.9 39.3 %all-gather.15.cloned.1.call-done = bf16[128,4096]{1,0:T(8,128)(2,1)} async-done(((bf16[128,512]{1,0:T(8,128)(2,1)}), bf16[128,4096]{1,0:T(8,128)(2,1)}) %all-gather.15.cloned.1.call-update) | async-done | bytes 1048592 | tf_op jit(solution)/shard_map/all_gather | solution.py:31
  410.2 4.7 fusion.10
  415.0 38.5 %all-gather.17.cloned.1.call-done = bf16[128,4096]{1,0:T(8,128)(2,1)} async-done(((bf16[128,512]{1,0:T(8,128)(2,1)}), bf16[128,4096]{1,0:T(8,128)(2,1)}) %all-gather.17.cloned.1.call-update) | async-done | bytes 1048592 | tf_op jit(solution)/shard_map/all_gather | solution.py:36
  459.5 63.8 %reduce-scatter.21.cloned.1.call-done = bf16[128,512]{1,0:T(8,128)(2,1)} async-done(((bf16[128,4096]{1,0:T(8,128)(2,1)}), bf16[128,512]{1,0:T(8,128)(2,1)}) %reduce-scatter.21.cloned.1.call-update) | async-done | bytes 131088 | tf_op jit(solution)/shard_map/reduce_scatter | solution.py:18
  527.4 63.8 %reduce-scatter.23.cloned.1.call-done = bf16[128,512]{1,0:T(8,128)(2,1)} async-done(((bf16[128,4096]{1,0:T(8,128)(2,1)}), bf16[128,512]{1,0:T(8,128)(2,1)}) %reduce-scatter.23.cloned.1.call-update) | async-done | bytes 131088 | tf_op jit(solution)/shard_map/reduce_scatter | solution.py:23
  592.9 39.3 %all-gather.19.cloned.1.call-done = bf16[128,4096]{1,0:T(8,128)(2,1)} async-done(((bf16[128,512]{1,0:T(8,128)(2,1)}), bf16[128,4096]{1,0:T(8,128)(2,1)}) %all-gather.19.cloned.1.call-update) | async-done | bytes 1048592 | tf_op jit(solution)/shard_map/all_gather | solution.py:31
  632.2 4.7 fusion.11
  637.2 38.3 %all-gather.21.cloned.1.call-done = bf16[128,4096]{1,0:T(8,128)(2,1)} async-done(((bf16[128,512]{1,0:T(8,128)(2,1)}), bf16[128,4096]{1,0:T(8,128)(2,1)}) %all-gather.21.cloned.1.call-update) | async-done | bytes 1048592 | tf_op jit(solution)/shard_map/all_gather | solution.py:36
  681.5 63.8 %reduce-scatter.25.cloned.1.call-done = bf16[128,512]{1,0:T(8,128)(2,1)} async-done(((bf16[128,4096]{1,0:T(8,128)(2,1)}), bf16[128,512]{1,0:T(8,128)(2,1)}) %reduce-scatter.25.cloned.1.call-update) | async-done | bytes 131088 | tf_op jit(solution)/shard_map/reduce_scatter | solution.py:18
  749.4 63.7 %reduce-scatter.27.cloned.1.call-done = bf16[128,512]{1,0:T(8,128)(2,1)} async-done(((bf16[128,4096]{1,0:T(8,128)(2,1)}), bf16[128,512]{1,0:T(8,128)(2,1)}) %reduce-scatter.27.cloned.1.call-update) | async-done | bytes 131088 | tf_op jit(solution)/shard_map/reduce_scatter | solution.py:23
  814.8 39.1 %all-gather.23.cloned.1.call-done = bf16[128,4096]{1,0:T(8,128)(2,1)} async-done(((bf16[128,512]{1,0:T(8,128)(2,1)}), bf16[128,4096]{1,0:T(8,128)(2,1)}) %all-gather.23.cloned.1.call-update) | async-done | bytes 1048592 | tf_op jit(solution)/shard_map/all_gather | solution.py:31
  853.9 4.7 fusion.12
  858.7 38.5 %all-gather.25.cloned.1.call-done = bf16[128,4096]{1,0:T(8,128)(2,1)} async-done(((bf16[128,512]{1,0:T(8,128)(2,1)}), bf16[128,4096]{1,0:T(8,128)(2,1)}) %all-gather.25.cloned.1.call-update) | async-done | bytes 1048592 | tf_op jit(solution)/shard_map/all_gather | solution.py:36
  904.2 68.0 %reduce-scatter.29.cloned.1.call-done = bf16[256,512]{1,0:T(8,128)(2,1)} async-done(((bf16[256,4096]{1,0:T(8,128)(2,1)}), bf16[256,512]{1,0:T(8,128)(2,1)}) %reduce-scatter.29.cloned.1.call-update) | async-done | bytes 262160 | tf_op jit(solution)/shard_map/reduce_scatter | solution.py:18
  972.1 4.9 convolution_convert_fusion
  977.1 68.0 %reduce-scatter.31.cloned.1.call-done = bf16[256,512]{1,0:T(8,128)(2,1)} async-done(((bf16[256,4096]{1,0:T(8,128)(2,1)}), bf16[256,512]{1,0:T(8,128)(2,1)}) %reduce-scatter.31.cloned.1.call-update) | async-done | bytes 262160 | tf_op jit(solution)/shard_map/reduce_scatter | solution.py:23
  1047.1 50.1 %all-gather.27.cloned.1.call-done = bf16[256,4096]{1,0:T(8,128)(2,1)} async-done(((bf16[256,512]{1,0:T(8,128)(2,1)}), bf16[256,4096]{1,0:T(8,128)(2,1)}) %all-gather.27.cloned.1.call-update) | async-done | bytes 2097168 | tf_op jit(solution)/shard_map/all_gather | solution.py:31
  1097.2 5.0 fusion
  1102.3 4.6 fusion.102
  1107.2 43.7 %all-gather.29.cloned.1.call-done = bf16[256,4096]{1,0:T(8,128)(2,1)} async-done(((bf16[256,512]{1,0:T(8,128)(2,1)}), bf16[256,4096]{1,0:T(8,128)(2,1)}) %all-gather.29.cloned.1.call-update) | async-done | bytes 2097168 | tf_op jit(solution)/shard_map/all_gather | solution.py:36
  1151.0 6.1 fusion.82
  1159.3 63.7 %reduce-scatter.35.cloned.1.call-done = f32[512,1024]{1,0:T(8,128)} async-done(((f32[512,4096]{1,0:T(8,128)}), f32[512,1024]{1,0:T(8,128)}) %reduce-scatter.35.cloned.1.call-update) | async-done | bytes 2097168 | tf_op jit(solution)/shard_map/reduce_scatter | solution.py:72
  1225.9 71.0 %reduce-scatter.33.cloned.1.call-done = f32[512,1024]{1,0:T(8,128)} async-done(((f32[512,4096]{1,0:T(8,128)}), f32[512,1024]{1,0:T(8,128)}) %reduce-scatter.33.cloned.1.call-update) | async-done | bytes 2097168 | tf_op jit(solution)/shard_map/reduce_scatter | solution.py:71
  1300.9 39.6 %all-reduce = (f32[]{:T(128)}, f32[]{:T(128)}) all-reduce(f32[]{:T(128)S(6)} %add.138, f32[]{:T(128)} %multiply_reduce_fusion.2), channel_id=1, replica_groups=mesh['dp'=4,'fsdp'=8] {'dp','fsdp'}, use_global_device_ids=true, to_apply=%region_14.15 | all-reduce | flops 2 | bytes 16 | tf_op jit(solution)/shard_map/psum | solution.py:76
  1341.8 4.2 broadcast_divide_fusion
  (100 shorter events, 62.6 us)
Async XLA Ops:
  7.2 72.3 %reduce-scatter.13.cloned.1.call-start = ((), (), s32[]{:S(2)}) async-start(), calls=%async_computation.12 | async-start | bytes 1179648 | tf_op jit(solution)/shard_map/reduce_scatter | solution.py:18
  11.2 136.1 %copy-start.15 = (f32[512]{0:T(512)S(1)}, f32[512]{0:T(512)}, u32[]{:S(2)}) copy-start(f32[512]{0:T(512)} %param.11) | copy-start | bytes 6148
  11.2 136.0 %reduce-scatter.15.cloned.1.call-start = ((), (), s32[]{:S(2)}) async-start(), calls=%async_computation.13 | async-start | bytes 1179648 | tf_op jit(solution)/shard_map/reduce_scatter | solution.py:23
  79.4 108.8 %copy-start.11 = (bf16[128,512]{1,0:T(8,128)(2,1)S(1)}, bf16[128,512]{1,0:T(8,128)(2,1)}, u32[]{:S(2)}) copy-start(bf16[128,512]{1,0:T(8,128)(2,1)} %reduce-scatter.13.cloned.1.call-done) | copy-start | bytes 393220
  83.4 148.1 %copy-start.6 = (f32[4,128,512]{2,1,0:T(8,128)S(1)}, f32[4,128,512]{2,1,0:T(8,128)}, u32[]{:S(2)}) copy-start(f32[4,128,512]{2,1,0:T(8,128)} %param.8) | copy-start | bytes 3145732
  83.4 148.1 %copy-start.7 = (f32[128,512]{1,0:T(8,128)S(1)}, f32[128,512]{1,0:T(8,128)}, u32[]{:S(2)}) copy-start(f32[128,512]{1,0:T(8,128)} %param.7) | copy-start | bytes 786436
  83.5 104.7 %all-gather.11.cloned.1.call-start = ((), (), s32[]{:S(2)}) async-start(), calls=%async_computation.14 | async-start | bytes 1179648 | tf_op jit(solution)/shard_map/all_gather | solution.py:31
  148.9 82.6 %all-gather.13.cloned.1.call-start = ((), (), s32[]{:S(2)}) async-start(), calls=%async_computation.15 | async-start | bytes 1179648 | tf_op jit(solution)/shard_map/all_gather | solution.py:36
  192.9 108.4 %reduce-scatter.17.cloned.1.call-start = ((), (), s32[]{:S(2)}) async-start(), calls=%async_computation.16 | async-start | bytes 1179648 | tf_op jit(solution)/shard_map/reduce_scatter | solution.py:18
  237.5 131.7 %reduce-scatter.19.cloned.1.call-start = ((), (), s32[]{:S(2)}) async-start(), calls=%async_computation.17 | async-start | bytes 1179648 | tf_op jit(solution)/shard_map/reduce_scatter | solution.py:23
  301.3 108.9 %copy-start.12 = (bf16[128,512]{1,0:T(8,128)(2,1)S(1)}, bf16[128,512]{1,0:T(8,128)(2,1)}, u32[]{:S(2)}) copy-start(bf16[128,512]{1,0:T(8,128)(2,1)} %reduce-scatter.17.cloned.1.call-done) | copy-start | bytes 393220
  305.3 104.9 %all-gather.15.cloned.1.call-start = ((), (), s32[]{:S(2)}) async-start(), calls=%async_computation.18 | async-start | bytes 1179648 | tf_op jit(solution)/shard_map/all_gather | solution.py:31
  370.9 82.6 %all-gather.17.cloned.1.call-start = ((), (), s32[]{:S(2)}) async-start(), calls=%async_computation.19 | async-start | bytes 1179648 | tf_op jit(solution)/shard_map/all_gather | solution.py:36
  414.9 108.4 %reduce-scatter.21.cloned.1.call-start = ((), (), s32[]{:S(2)}) async-start(), calls=%async_computation.20 | async-start | bytes 1179648 | tf_op jit(solution)/shard_map/reduce_scatter | solution.py:18
  459.4 131.8 %reduce-scatter.23.cloned.1.call-start = ((), (), s32[]{:S(2)}) async-start(), calls=%async_computation.21 | async-start | bytes 1179648 | tf_op jit(solution)/shard_map/reduce_scatter | solution.py:23
  523.3 108.9 %copy-start.13 = (bf16[128,512]{1,0:T(8,128)(2,1)S(1)}, bf16[128,512]{1,0:T(8,128)(2,1)}, u32[]{:S(2)}) copy-start(bf16[128,512]{1,0:T(8,128)(2,1)} %reduce-scatter.21.cloned.1.call-done) | copy-start | bytes 393220
  527.3 104.9 %all-gather.19.cloned.1.call-start = ((), (), s32[]{:S(2)}) async-start(), calls=%async_computation.22 | async-start | bytes 1179648 | tf_op jit(solution)/shard_map/all_gather | solution.py:31
  592.9 82.6 %all-gather.21.cloned.1.call-start = ((), (), s32[]{:S(2)}) async-start(), calls=%async_computation.23 | async-start | bytes 1179648 | tf_op jit(solution)/shard_map/all_gather | solution.py:36
  636.9 108.4 %reduce-scatter.25.cloned.1.call-start = ((), (), s32[]{:S(2)}) async-start(), calls=%async_computation.24 | async-start | bytes 1179648 | tf_op jit(solution)/shard_map/reduce_scatter | solution.py:18
  681.4 131.6 %reduce-scatter.27.cloned.1.call-start = ((), (), s32[]{:S(2)}) async-start(), calls=%async_computation.25 | async-start | bytes 1179648 | tf_op jit(solution)/shard_map/reduce_scatter | solution.py:23
  745.3 108.6 %copy-start.14 = (bf16[128,512]{1,0:T(8,128)(2,1)S(1)}, bf16[128,512]{1,0:T(8,128)(2,1)}, u32[]{:S(2)}) copy-start(bf16[128,512]{1,0:T(8,128)(2,1)} %reduce-scatter.25.cloned.1.call-done) | copy-start | bytes 393220
  749.3 104.6 %all-gather.23.cloned.1.call-start = ((), (), s32[]{:S(2)}) async-start(), calls=%async_computation.26 | async-start | bytes 1179648 | tf_op jit(solution)/shard_map/all_gather | solution.py:31
  814.8 82.5 %all-gather.25.cloned.1.call-start = ((), (), s32[]{:S(2)}) async-start(), calls=%async_computation.27 | async-start | bytes 1179648 | tf_op jit(solution)/shard_map/all_gather | solution.py:36
  858.6 113.5 %reduce-scatter.29.cloned.1.call-start = ((), (), s32[]{:S(2)}) async-start(), calls=%async_computation.28 | async-start | bytes 2359296 | tf_op jit(solution)/shard_map/reduce_scatter | solution.py:18
  904.1 141.1 %copy-start.16 = (f32[256]{0:T(256)S(1)}, f32[256]{0:T(256)}, u32[]{:S(2)}) copy-start(f32[256]{0:T(256)} %constant.24.clone.1) | copy-start | bytes 3076
  904.1 141.1 %reduce-scatter.31.cloned.1.call-start = ((), (), s32[]{:S(2)}) async-start(), calls=%async_computation.29 | async-start | bytes 2359296 | tf_op jit(solution)/shard_map/reduce_scatter | solution.py:23
  972.1 125.1 %copy-start.9 = (bf16[256,512]{1,0:T(8,128)(2,1)S(1)}, bf16[256,512]{1,0:T(8,128)(2,1)}, u32[]{:S(2)}) copy-start(bf16[256,512]{1,0:T(8,128)(2,1)} %reduce-scatter.29.cloned.1.call-done) | copy-start | bytes 786436
  977.1 120.1 %all-gather.27.cloned.1.call-start = ((), (), s32[]{:S(2)}) async-start(), calls=%async_computation.30 | async-start | bytes 2359296 | tf_op jit(solution)/shard_map/all_gather | solution.py:31
  1047.1 103.9 %all-gather.29.cloned.1.call-start = ((), (), s32[]{:S(2)}) async-start(), calls=%async_computation.31 | async-start | bytes 2359296 | tf_op jit(solution)/shard_map/all_gather | solution.py:36
  1102.3 120.7 %reduce-scatter.35.cloned.1.call-start = ((), (), s32[]{:S(2)}) async-start(), calls=%async_computation.33 | async-start | bytes 10485760 | tf_op jit(solution)/shard_map/reduce_scatter | solution.py:72
  1107.0 189.9 %reduce-scatter.33.cloned.1.call-start = ((), (), s32[]{:S(2)}) async-start(), calls=%async_computation.32 | async-start | bytes 10485760 | tf_op jit(solution)/shard_map/reduce_scatter | solution.py:71
  1223.0 118.8 %copy-start.4 = (f32[512,1024]{1,0:T(8,128)S(1)}, f32[512,1024]{1,0:T(8,128)}, u32[]{:S(2)}) copy-start(f32[512,1024]{1,0:T(8,128)} %reduce-scatter.35.cloned.1.call-done) | copy-start | bytes 6291460
  (7 other events, 65.7 us)
Sparse Core Ops, SparseCore 0:
  11.9 67.4 reduce-scatter.12
  83.6 63.6 reduce-scatter.14
  149.9 38.2 all-gather.10
  193.1 38.3 all-gather.12
  237.6 63.6 reduce-scatter.16
  305.5 63.6 reduce-scatter.18
  371.8 38.3 all-gather.14
  415.0 38.3 all-gather.16
  459.5 63.7 reduce-scatter.20
  527.5 63.6 reduce-scatter.22
  593.8 38.3 all-gather.18
  637.1 38.3 all-gather.20
  681.6 63.6 reduce-scatter.24
  749.4 63.5 reduce-scatter.26
  815.5 38.3 all-gather.22
  858.8 38.3 all-gather.24
  904.2 67.8 reduce-scatter.28
  977.2 67.9 reduce-scatter.30
  1047.8 49.3 all-gather.26
  1102.4 48.5 all-gather.28
  1153.5 69.4 reduce-scatter.34
  1225.6 71.2 reduce-scatter.32
where the time goes:
time: 1350 us
  waiting for transfers between devices  1190 us (88%)
  matrix products  84.5 us (6%)
  blocking collectives  39.6 us (3%)
  other arithmetic  19 us (1%)
  between operations  18.3 us (1%)
    reduce_scatter x5, waiting for transfers between devices, forward(): lax.psum_scatter(term_one.astype(jnp.bfloat16), 'fsdp', scatter_dimension...  328 us
    reduce_scatter x5, waiting for transfers between devices, forward(): lax.psum_scatter(term_two.astype(jnp.bfloat16), 'fsdp', scatter_dimension...  323 us
    all_gather x5, waiting for transfers between devices, backward(): full_two = lax.all_gather(grad_two, 'fsdp', axis=1, tiled=True)  207 us
    all_gather x5, waiting for transfers between devices, backward(): full_one = lax.all_gather(grad_one, 'fsdp', axis=1, tiled=True)  198 us
    reduce_scatter x1, waiting for transfers between devices, local(): lax.psum_scatter(raw_one, 'dp', scatter_dimension=1, tiled=True)  71 us
    reduce_scatter x1, waiting for transfers between devices, local(): lax.psum_scatter(raw_two, 'dp', scatter_dimension=1, tiled=True)  63.7 us
    psum x1, blocking collectives, local(): square_total = lax.psum(squares, ('dp', 'fsdp'))  39.6 us
  transfers between devices with their start and end apart: 22, of which 22 were waited for; matrix products, arithmetic and copies ran while one was open for 1% of the time, Pallas kernels for 0%

commit v1 on v0

v1 whole, which is shorter than its diff:
```python
import functools

import jax
import jax.numpy as jnp
from jax import lax
from jax.experimental import pallas as pl
from jax.experimental.pallas import tpu as pltpu
from jax.sharding import PartitionSpec as P

MESH = pl.DeviceIdType.MESH
BF16 = jnp.bfloat16
F32 = jnp.float32


def inner_of(n):
    return max(i for i in range(1, n + 1) if n % i == 0 and i * i <= n)


def folded(values):
    rows, columns = values.shape
    tall = values.reshape(rows // 8, 8, columns).sum(axis=0)
    out = tall[:, :128]
    for at in range(128, columns, 128):
        out += tall[:, at : at + 128]
    return out


def kernel(
    n, X, dpn, steps,
    data_ref, start_ref, noise_ref, w1_ref, w2_ref, read_ref,
    raw1_ref, raw2_ref, stat_ref,
    state, s_a, r_a, s_b, r_b, acc, ag_data, ag_neg, rows_all, hid_all, g_all, own_stat, got_stat,
    sem_as, sem_ar, sem_bs, sem_br, sem_zs, sem_zr, sem_xs, sem_xr, sem_ds, sem_dr, sem_ts, sem_tr,
):
    Z = n // X
    q = n // dpn
    C = w1_ref.shape[1] // n
    me = lax.axis_index("fsdp")
    dpi = lax.axis_index("dp")
    z, x = me // X, me % X

    def dest(oz, ox):
        return ((z + oz) % Z) * X + (x + ox) % X

    def source(oz, ox):
        return ((z + Z - oz) % Z) * X + (x + X - ox) % X

    def dp_dest(o):
        return (dpi + o) % dpn

    def cols(at):
        return pl.ds(pl.multiple_of(at * C, C), C)

    def send(src, dst, ssem, rsem, axis, peer):
        return pltpu.make_async_remote_copy(
            src_ref=src, dst_ref=dst, send_sem=ssem, recv_sem=rsem,
            device_id={axis: peer}, device_id_type=MESH,
        )

    partners = (
        [("fsdp", dest(0, ox)) for ox in range(1, X)]
        + [("fsdp", dest(oz, 0)) for oz in range(1, Z)]
        + [("dp", dp_dest(o)) for o in range(1, dpn)]
    )
    barrier = pltpu.get_barrier_semaphore()
    for axis, peer in partners:
        pl.semaphore_signal(barrier, inc=1, device_id={axis: peer}, device_id_type=MESH)
    pl.semaphore_wait(barrier, len(partners))

    def settle(copies):
        for copy in copies:
            copy.wait_send()

    def reduce_scatter(j, lhs, w_ref):
        sent, from_x, from_z = [], {}, {}
        order = list(range(1, Z)) + [0]
        for oz in order:
            for ox in range(1, X):
                s_a[j, oz, ox - 1] = jnp.dot(
                    lhs, w_ref[:, cols(dest(oz, ox))], preferred_element_type=F32
                ).astype(BF16)
                copy = send(
                    s_a.at[j, oz, ox - 1], r_a.at[j, oz, ox - 1],
                    sem_as.at[j, oz, ox - 1], sem_ar.at[j, oz, ox - 1], "fsdp", dest(0, ox),
                )
                copy.start()
                sent.append(copy)
                from_x[oz, ox] = copy
        for oz in order:
            acc[oz] = jnp.dot(lhs, w_ref[:, cols(dest(oz, 0))], preferred_element_type=F32)

        def joined(oz):
            total = acc[oz]
            for ox in range(1, X):
                from_x[oz, ox].wait_recv()
                total += r_a[j, oz, ox - 1].astype(F32)
            return total

        for oz in range(1, Z):
            s_b[j, oz - 1] = joined(oz).astype(BF16)
            copy = send(
                s_b.at[j, oz - 1], r_b.at[j, oz - 1],
                sem_bs.at[j, oz - 1], sem_br.at[j, oz - 1], "fsdp", dest(oz, 0),
            )
            copy.start()
            sent.append(copy)
            from_z[oz] = copy
        total = joined(0)
        for oz in range(1, Z):
            from_z[oz].wait_recv()
            total += r_b[j, oz - 1].astype(F32)
        return total, sent

    def gather_dot(j, buf, w_ref):
        sent = []

        def block(at):
            return lax.dot_general(
                buf[at], w_ref[:, cols(at)], (((1,), (1,)), ((), ())), preferred_element_type=F32
            )

        def push(at, ssem, rsem, peer):
            copy = send(buf.at[at], buf.at[at], ssem, rsem, "fsdp", peer)
            copy.start()
            sent.append(copy)

        def arrive(at, ssem, rsem):
            send(buf.at[at], buf.at[at], ssem, rsem, "fsdp", dest(1, 0)).wait_recv()

        for oz in range(1, Z):
            push(me, sem_zs.at[j, oz - 1], sem_zr.at[j, oz - 1], dest(oz, 0))
        for ox in range(1, X):
            push(me, sem_xs.at[j, 0, ox - 1], sem_xr.at[j, 0, ox - 1], dest(0, ox))
        total = block(me)
        for oz in range(1, Z):
            at = source(oz, 0)
            arrive(at, sem_zs.at[j, oz - 1], sem_zr.at[j, oz - 1])
            for ox in range(1, X):
                push(at, sem_xs.at[j, oz, ox - 1], sem_xr.at[j, oz, ox - 1], dest(0, ox))
            total += block(at)
        for oz in range(Z):
            for ox in range(1, X):
                at = source(oz, ox)
                arrive(at, sem_xs.at[j, oz, ox - 1], sem_xr.at[j, oz, ox - 1])
                total += block(at)
        return total, sent

    def slope(a):
        s = jax.nn.sigmoid(a)
        return s * (1.0 + a * (1.0 - s))

    def one_pass(u, sign, buf, keep):
        a1, sent_1 = reduce_scatter(0, u, w1_ref)
        s1 = jax.nn.sigmoid(a1)
        hidden = (a1 * s1).astype(BF16)
        slope_1 = s1 * (1.0 + a1 * (1.0 - s1))
        a2, sent_2 = reduce_scatter(1, hidden, w2_ref)
        settle(sent_1)
        g2 = (sign * read_ref[...] * slope(a2)).astype(BF16)
        buf[0, me] = g2
        back, sent_3 = gather_dot(0, buf.at[0], w2_ref)
        settle(sent_2)
        buf[1, me] = (back * slope_1).astype(BF16)
        waits = keep(0, u, hidden, a2)
        moved, sent_4 = gather_dot(1, buf.at[1], w1_ref)
        waits += keep(1, u, hidden, a2)
        settle(sent_3 + sent_4)
        return moved, waits

    def exchange(half, buf, stage, u, hidden, a2):
        sent = []

        def to_peers(kind, pick, dst):
            for o in range(1, dpn):
                copy = send(
                    pick(dp_dest(o)), dst, sem_ds.at[half, kind, o - 1], sem_dr.at[half, kind, o - 1],
                    "dp", dp_dest(o),
                )
                copy.start()
                sent.append(copy)

        if stage == 0:
            rows_all[half, dpi] = u
            hid_all[half, dpi] = hidden
            to_peers(0, lambda d: rows_all.at[half, dpi], rows_all.at[half, dpi])
            to_peers(1, lambda d: hid_all.at[half, dpi], hid_all.at[half, dpi])
        g = 0 if stage == 0 else 1
        for k in range(q):
            g_all[half, g, k, dpi] = buf[g, dpi * q + k]
            to_peers(2 + g * q + k, lambda d, k=k: buf.at[g, d * q + k], g_all.at[half, g, k, dpi])
        if stage == 0:
            energy = folded(read_ref[...] * (a2 * jax.nn.sigmoid(a2)))
            own_stat[0] = energy if half == 0 else own_stat[0] - energy
        return sent

    def nothing(stage, u, hidden, a2):
        return []

    moved, sent_data = one_pass(data_ref[...], 1.0, ag_data, functools.partial(exchange, 0, ag_data))

    state[...] = start_ref[...]

    def langevin(step, carry):
        moved, _ = one_pass(state[...].astype(BF16), 1.0, ag_neg, nothing)
        state[...] = state[...] - 0.005 * moved + 0.1 * noise_ref[step]
        return carry

    lax.fori_loop(0, steps, langevin, 0)

    moved, sent_neg = one_pass(
        state[...].astype(BF16), -1.0, ag_neg, functools.partial(exchange, 1, ag_neg)
    )

    def arrived(half, kinds):
        for kind in kinds:
            for o in range(1, dpn):
                at = (dpi + dpn - o) % dpn
                if kind == 0:
                    ref = rows_all.at[half, at]
                elif kind == 1:
                    ref = hid_all.at[half, at]
                else:
                    ref = g_all.at[half, (kind - 2) // q, (kind - 2) % q, at]
                send(
                    ref, ref, sem_ds.at[half, kind, o - 1], sem_dr.at[half, kind, o - 1],
                    "dp", dp_dest(o),
                ).wait_recv()

    for half in range(2):
        arrived(half, range(2 + 2 * q))

    def contract(left, right):
        return lax.dot_general(
            left.reshape(-1, left.shape[-1]), right.reshape(-1, right.shape[-1]),
            (((0,), (0,)), ((), ())), preferred_element_type=F32,
        )

    squares = jnp.zeros((8, 128), F32)
    for g, left, out_ref in ((1, rows_all, raw1_ref), (0, hid_all, raw2_ref)):
        for k in range(q):
            raw = contract(left[0], g_all[0, g, k]) + contract(left[1], g_all[1, g, k])
            out_ref[:, k * C : (k + 1) * C] = raw
            squares += folded(raw * raw)
    own_stat[1] = squares

    settle(sent_data + sent_neg)

    base = 0
    for axis, count, peer in (
        ("fsdp", X, lambda o: dest(0, o)), ("fsdp", Z, lambda o: dest(o, 0)), ("dp", dpn, dp_dest),
    ):
        copies = []
        for o in range(1, count):
            at = base + o - 1
            copy = send(own_stat, got_stat.at[at], sem_ts.at[at], sem_tr.at[at], axis, peer(o))
            copy.start()
            copies.append(copy)
        total = own_stat[...]
        for o, copy in enumerate(copies):
            copy.wait()
            total += got_stat[base + o]
        own_stat[...] = total
        base += count - 1
    stat_ref[...] = own_stat[...]


def solution(mesh):
    n, dpn = mesh.shape["fsdp"], mesh.shape["dp"]
    X = inner_of(n)
    Z = n // X
    q = n // dpn

    def local(data, start, noise, w1, w2, readout):
        R, K = start.shape
        H = w1.shape[1]
        C = H // n
        steps = noise.shape[0]
        vmem = pl.BlockSpec(memory_space=pltpu.VMEM)
        dma = pltpu.SemaphoreType.DMA
        kinds = 2 + 2 * q
        peers = (X - 1) + (Z - 1) + (dpn - 1)
        raw1, raw2, stat = pl.pallas_call(
            functools.partial(kernel, n, X, dpn, steps),
            name="contrastive",
            out_shape=(
                jax.ShapeDtypeStruct((K, q * C), F32),
                jax.ShapeDtypeStruct((C, q * C), F32),
                jax.ShapeDtypeStruct((2, 8, 128), F32),
            ),
            in_specs=[vmem] * 6,
            out_specs=(vmem,) * 3,
            scratch_shapes=[
                pltpu.VMEM((R, K), F32),
                pltpu.VMEM((2, Z, X - 1, R, C), BF16),
                pltpu.VMEM((2, Z, X - 1, R, C), BF16),
                pltpu.VMEM((2, Z - 1, R, C), BF16),
                pltpu.VMEM((2, Z - 1, R, C), BF16),
                pltpu.VMEM((Z, R, C), F32),
                pltpu.VMEM((2, n, R, C), BF16),
                pltpu.VMEM((2, n, R, C), BF16),
                pltpu.VMEM((2, dpn, R, K), BF16),
                pltpu.VMEM((2, dpn, R, C), BF16),
                pltpu.VMEM((2, 2, q, dpn, R, C), BF16),
                pltpu.VMEM((2, 8, 128), F32),
                pltpu.VMEM((peers, 2, 8, 128), F32),
                dma((2, Z, X - 1)), dma((2, Z, X - 1)),
                dma((2, Z - 1)), dma((2, Z - 1)),
                dma((2, Z - 1)), dma((2, Z - 1)),
                dma((2, Z, X - 1)), dma((2, Z, X - 1)),
                dma((2, kinds, dpn - 1)), dma((2, kinds, dpn - 1)),
                dma((peers,)), dma((peers,)),
            ],
            compiler_params=pltpu.CompilerParams(
                collective_id=0, has_side_effects=True, vmem_limit_bytes=60 * 1024 * 1024
            ),
        )(data, start, noise, w1, w2, readout.reshape(1, C))
        sums = jnp.sum(stat, axis=(1, 2))
        energy_gap = sums[0] / (R * dpn * 80.0 * jnp.sqrt(jnp.float32(H)))
        scale = jnp.sqrt(sums[1] / (2.0 * (K * n) * H) + 1e-06)
        return raw1 / scale, raw2 / scale, energy_gap

    in_specs = (
        P("dp", "fsdp"),
        P("dp", "fsdp"),
        P(None, "dp", "fsdp"),
        P("fsdp", None),
        P("fsdp", None),
        P("fsdp"),
    )
    out_specs = (P("fsdp", "dp"), P("fsdp", "dp"), P())
    return jax.shard_map(local, mesh=mesh, in_specs=in_specs, out_specs=out_specs, check_vma=False)
```

time: 1350 us -> 433 us (0.32)
  waiting for transfers between devices: 1190 us -> 0 us
  Pallas kernels: 0 us -> 423 us
  matrix products: 84.5 us -> 0 us
  blocking collectives: 39.6 us -> 0 us
  between operations: 18.3 us -> 3.11 us
    reduce_scatter x12 -> x0, waiting for transfers between devices: 785 us -> none  [the longest x5 328 us: forward(): lax.psum_scatter(term_one.astype(jnp.bfloat16), 'fsdp', scatter_dimension...]
    pallas_call x0 -> x1, Pallas kernels: none -> 423 us  [local(): pl.pallas_call(functools.partial(kernel, n, X, dpn, steps), name='contras...]
    all_gather x10 -> x0, waiting for transfers between devices: 405 us -> none  [the longest x5 207 us: backward(): full_two = lax.all_gather(grad_two, 'fsdp', axis=1, tiled=True)]
    dot_general x22 -> x0, matrix products: 84.5 us -> none  [the longest x5 23.8 us: backward(): lax.dot_general(full_two, second_weight, (((1,), (1,)), ((), ())), prefer...]
    psum x1 -> x0, blocking collectives: 39.6 us -> none  [local(): square_total = lax.psum(squares, ('dp', 'fsdp'))]
  transfers between devices with their start and end apart: 22 -> 0, of which waited for: 22 -> 0; matrix products, arithmetic and copies ran while one was open for 1% -> 0% of each run, Pallas kernels for 0% -> 0%
where the time goes in v1:
time: 433 us
  Pallas kernels  423 us (98%)
  other arithmetic  5.86 us (1%)
    pallas_call x1, Pallas kernels, local(): pl.pallas_call(functools.partial(kernel, n, X, dpn, steps), name='contras...  423 us

profile of v1, /device:TPU:0, one launch (start us, length us, event | category | flops | bytes accessed | tf_op | source)
XLA Modules:
  0.0 433.0 jit_solution(9393228434785695373)
XLA Ops:
  0.6 423.4 %contrastive.1 = (f32[512,1024]{1,0:T(8,128)}, f32[512,1024]{1,0:T(8,128)}, f32[2,8,128]{2,1,0:T(8,128)}) custom-call(bf16[128,512]{1,0:T(8,128)(2,1)} %data_ref.1, f32[128,512]{1,0:T(8,128)} %start_ref.1, f32[4,128,512]{2,1,0:T(8,128)} %noise_ref.1, bf16[512,4096]{1,0:T(8,128)(2,1)} %w1_ref.1, bf16[512,4096]{1,0:T(8,128)(2,1)} %w2_ref.1, f32[1,512]{1,0:T(1,128)} %bitcast.3), custom_call_target="tpu_custom_call" | custom-call | tf_op jit(solution)/shard_map/contrastive/pallas_call | solution.py:282
  424.0 0.8 reduce_sum.9
  424.8 0.6 fusion
  426.8 5.1 %broadcast_divide_fusion = (f32[512,1024]{1,0:T(8,128)}, f32[512,1024]{1,0:T(8,128)}) fusion(f32[512,1024]{1,0:T(8,128)} %get-tuple-element.8, f32[]{:T(128)} %bitcast.1, f32[512,1024]{1,0:T(8,128)} %get-tuple-element.6), kind=kLoop, calls=%fused_computation | loop fusion | flops 1048576 | bytes 8388612 | tf_op jit(solution)/shard_map/div | solution.py:320

commit v2 on v1

v2 whole, which is shorter than its diff:
```python
import functools

import jax
import jax.numpy as jnp
from jax import lax
from jax.experimental import pallas as pl
from jax.experimental.pallas import tpu as pltpu
from jax.sharding import PartitionSpec as P

MESH = pl.DeviceIdType.MESH
BF16 = jnp.bfloat16
F32 = jnp.float32


def inner_of(n):
    return max(i for i in range(1, n + 1) if n % i == 0 and i * i <= n)


def folded(values):
    rows, columns = values.shape
    tall = values.reshape(rows // 8, 8, columns).sum(axis=0)
    out = tall[:, :128]
    for at in range(128, columns, 128):
        out += tall[:, at : at + 128]
    return out


def kernel(
    n, X, dpn, steps, S,
    data_ref, start_ref, noise_ref, w1_ref, w2_ref, read_ref,
    raw1_ref, raw2_ref, stat_ref,
    state, s_a, r_a, s_b, r_b, acc, ag_data, ag_neg, rows_all, hid_all, g_all, own_stat, got_stat,
    sem_as, sem_ar, sem_bs, sem_br, sem_zs, sem_zr, sem_xs, sem_xr, sem_ds, sem_dr, sem_ts, sem_tr,
):
    Z = n // X
    q = n // dpn
    C = w1_ref.shape[1] // n
    height = data_ref.shape[0] // S
    me = lax.axis_index("fsdp")
    dpi = lax.axis_index("dp")
    z, x = me // X, me % X

    def dest(oz, ox):
        return ((z + oz) % Z) * X + (x + ox) % X

    def source(oz, ox):
        return ((z + Z - oz) % Z) * X + (x + X - ox) % X

    def dp_dest(o):
        return (dpi + o) % dpn

    def cols(at):
        return pl.ds(pl.multiple_of(at * C, C), C)

    def send(src, dst, ssem, rsem, axis, peer):
        return pltpu.make_async_remote_copy(
            src_ref=src, dst_ref=dst, send_sem=ssem, recv_sem=rsem,
            device_id={axis: peer}, device_id_type=MESH,
        )

    partners = (
        [("fsdp", dest(0, ox)) for ox in range(1, X)]
        + [("fsdp", dest(oz, 0)) for oz in range(1, Z)]
        + [("dp", dp_dest(o)) for o in range(1, dpn)]
    )
    barrier = pltpu.get_barrier_semaphore()
    for axis, peer in partners:
        pl.semaphore_signal(barrier, inc=1, device_id={axis: peer}, device_id_type=MESH)
    pl.semaphore_wait(barrier, len(partners))

    def a_copy(s, j, oz, ox):
        return send(
            s_a.at[s, j, oz, ox - 1], r_a.at[s, j, oz, ox - 1],
            sem_as.at[s, j, oz, ox - 1], sem_ar.at[s, j, oz, ox - 1], "fsdp", dest(0, ox),
        )

    def b_copy(s, j, oz):
        return send(
            s_b.at[s, j, oz - 1], r_b.at[s, j, oz - 1],
            sem_bs.at[s, j, oz - 1], sem_br.at[s, j, oz - 1], "fsdp", dest(oz, 0),
        )

    def z_copy(s, j, oz, buf, at):
        ref = buf.at[s, j, at]
        return send(ref, ref, sem_zs.at[s, j, oz - 1], sem_zr.at[s, j, oz - 1], "fsdp", dest(oz, 0))

    def x_copy(s, j, oz, ox, buf, at):
        ref = buf.at[s, j, at]
        return send(
            ref, ref, sem_xs.at[s, j, oz, ox - 1], sem_xr.at[s, j, oz, ox - 1], "fsdp", dest(0, ox)
        )

    def scatter_open(s, j, lhs, w_ref):
        order = list(range(1, Z)) + [0]
        for oz in order:
            for ox in range(1, X):
                s_a[s, j, oz, ox - 1] = jnp.dot(
                    lhs, w_ref[:, cols(dest(oz, ox))], preferred_element_type=F32
                ).astype(BF16)
                a_copy(s, j, oz, ox).start()
        for oz in order:
            acc[s, oz] = jnp.dot(lhs, w_ref[:, cols(dest(oz, 0))], preferred_element_type=F32)

    def joined(s, j, oz):
        total = acc[s, oz]
        for ox in range(1, X):
            a_copy(s, j, oz, ox).wait_recv()
            total += r_a[s, j, oz, ox - 1].astype(F32)
        return total

    def scatter_join(s, j):
        for oz in range(1, Z):
            s_b[s, j, oz - 1] = joined(s, j, oz).astype(BF16)
            b_copy(s, j, oz).start()

    def scatter_close(s, j):
        total = joined(s, j, 0)
        for oz in range(1, Z):
            b_copy(s, j, oz).wait_recv()
            total += r_b[s, j, oz - 1].astype(F32)
        return total

    def scatter_settle(s, j):
        for oz in range(Z):
            for ox in range(1, X):
                a_copy(s, j, oz, ox).wait_send()
        for oz in range(1, Z):
            b_copy(s, j, oz).wait_send()

    def gather_open(s, j, buf):
        for oz in range(1, Z):
            z_copy(s, j, oz, buf, me).start()
        for ox in range(1, X):
            x_copy(s, j, 0, ox, buf, me).start()

    def block(s, j, buf, at, w_ref):
        return lax.dot_general(
            buf[s, j, at], w_ref[:, cols(at)], (((1,), (1,)), ((), ())), preferred_element_type=F32
        )

    def gather_forward(s, j, buf, w_ref):
        total = None if w_ref is None else block(s, j, buf, me, w_ref)
        for oz in range(1, Z):
            at = source(oz, 0)
            z_copy(s, j, oz, buf, at).wait_recv()
            for ox in range(1, X):
                x_copy(s, j, oz, ox, buf, at).start()
            if w_ref is not None:
                total += block(s, j, buf, at, w_ref)
        return total

    def gather_close(s, j, buf, w_ref, total):
        for oz in range(Z):
            for ox in range(1, X):
                at = source(oz, ox)
                x_copy(s, j, oz, ox, buf, at).wait_recv()
                if w_ref is not None:
                    total += block(s, j, buf, at, w_ref)
        return total

    def gather_settle(s, j, buf):
        for oz in range(1, Z):
            z_copy(s, j, oz, buf, me).wait_send()
        for oz in range(Z):
            for ox in range(1, X):
                x_copy(s, j, oz, ox, buf, source(oz, 0)).wait_send()

    def stages(s, u, sign, buf, keep, after, w_back):
        scatter_join(s, 0)
        yield
        a1 = scatter_close(s, 0)
        s1 = jax.nn.sigmoid(a1)
        hidden = (a1 * s1).astype(BF16)
        slope_1 = s1 * (1.0 + a1 * (1.0 - s1))
        scatter_open(s, 1, hidden, w2_ref)
        scatter_settle(s, 0)
        yield
        scatter_join(s, 1)
        yield
        a2 = scatter_close(s, 1)
        s2 = jax.nn.sigmoid(a2)
        buf[s, 0, me] = (sign * read_ref[...] * (s2 * (1.0 + a2 * (1.0 - s2)))).astype(BF16)
        gather_open(s, 0, buf)
        scatter_settle(s, 1)
        yield
        total = gather_forward(s, 0, buf, w2_ref)
        yield
        back = gather_close(s, 0, buf, w2_ref, total)
        buf[s, 1, me] = (back * slope_1).astype(BF16)
        gather_open(s, 1, buf)
        keep(s, 0, u, hidden, a2 * s2)
        yield
        total = gather_forward(s, 1, buf, w_back)
        yield
        moved = gather_close(s, 1, buf, w_back, total)
        keep(s, 1, u, hidden, None)
        gather_settle(s, 0, buf)
        gather_settle(s, 1, buf)
        after(s, moved)

    def interleave(passes):
        passes = list(passes)
        while passes:
            passes = [p for p in passes if next(p, passes) is not passes]

    def dp_ref(half, kind, d, s):
        if kind == 0:
            return rows_all.at[half, d, s]
        if kind == 1:
            return hid_all.at[half, d, s]
        return g_all.at[half, (kind - 2) // q, (kind - 2) % q, d, s]

    def dp_copy(half, kind, o, s, src, d):
        return send(
            src, dp_ref(half, kind, d, s), sem_ds.at[half, kind, o - 1, s],
            sem_dr.at[half, kind, o - 1, s], "dp", dp_dest(o),
        )

    def dp_copies(half, buf, s, stage):
        kinds = ([0, 1] if stage == 0 else []) + [2 + stage * q + k for k in range(q)]
        for kind in kinds:
            for o in range(1, dpn):
                if kind < 2:
                    own = dp_ref(half, kind, dpi, s)
                else:
                    own = buf.at[s, stage, dp_dest(o) * q + (kind - 2) % q]
                yield dp_copy(half, kind, o, s, own, dpi)

    def exchange(half, buf, s, stage, u, hidden, silu_2):
        if stage == 0:
            rows_all[half, dpi, s] = u
            hid_all[half, dpi, s] = hidden
            energy = folded(read_ref[...] * silu_2)
            if half == 0 and s == 0:
                own_stat[0] = energy
            else:
                own_stat[0] = own_stat[0] + energy if half == 0 else own_stat[0] - energy
        for k in range(q):
            g_all[half, stage, k, dpi, s] = buf[s, stage, dpi * q + k]
        for copy in dp_copies(half, buf, s, stage):
            copy.start()

    def nothing(*args):
        return None

    def rows_of(s):
        return pl.ds(s * height, height)

    def opened(s, *args):
        scatter_open(s, 0, state[rows_of(s), :].astype(BF16), w1_ref)

    streams = range(S)
    for s in streams:
        scatter_open(s, 0, data_ref[rows_of(s), :], w1_ref)
    state[...] = start_ref[...]
    interleave(
        stages(
            s, data_ref[rows_of(s), :], 1.0, ag_data, functools.partial(exchange, 0, ag_data), opened, None
        )
        for s in streams
    )

    def langevin(step, carry):
        def after(s, moved):
            at = rows_of(s)
            state[at, :] = state[at, :] - 0.005 * moved + 0.1 * noise_ref[step, at, :]
            opened(s)

        interleave(stages(s, None, 1.0, ag_neg, nothing, after, w1_ref) for s in streams)
        return carry

    lax.fori_loop(0, steps, langevin, 0)

    def contract(left, right):
        return lax.dot_general(
            left.reshape(-1, left.shape[-1]), right.reshape(-1, right.shape[-1]),
            (((0,), (0,)), ((), ())), preferred_element_type=F32,
        )

    def arrived(half, kinds):
        for s in streams:
            for kind in kinds:
                for o in range(1, dpn):
                    at = (dpi + dpn - o) % dpn
                    dp_copy(half, kind, o, s, dp_ref(half, kind, at, s), at).wait_recv()

    def gradients():
        for _ in range(6):
            yield
        arrived(0, range(2 + 2 * q))
        for g, left, out_ref in ((1, rows_all, raw1_ref), (0, hid_all, raw2_ref)):
            for k in range(q):
                out_ref[:, k * C : (k + 1) * C] = contract(left[0], g_all[0, g, k])

    interleave(
        [
            stages(
                s, state[rows_of(s), :].astype(BF16), -1.0, ag_neg,
                functools.partial(exchange, 1, ag_neg), nothing, None,
            )
            for s in streams
        ]
        + [gradients()]
    )

    squares = jnp.zeros((8, 128), F32)
    for g, left, out_ref in ((0, hid_all, raw2_ref), (1, rows_all, raw1_ref)):
        arrived(1, ([0, 1] if g == 0 else []) + [2 + g * q + k for k in range(q)])
        for k in range(q):
            at = slice(k * C, (k + 1) * C)
            raw = out_ref[:, at] + contract(left[1], g_all[1, g, k])
            out_ref[:, at] = raw
            squares += folded(raw * raw)
    own_stat[1] = squares

    for half, buf in ((0, ag_data), (1, ag_neg)):
        for s in streams:
            for stage in range(2):
                for copy in dp_copies(half, buf, s, stage):
                    copy.wait_send()

    base = 0
    for axis, count, peer in (
        ("fsdp", X, lambda o: dest(0, o)), ("fsdp", Z, lambda o: dest(o, 0)), ("dp", dpn, dp_dest),
    ):
        copies = []
        for o in range(1, count):
            at = base + o - 1
            copy = send(own_stat, got_stat.at[at], sem_ts.at[at], sem_tr.at[at], axis, peer(o))
            copy.start()
            copies.append(copy)
        total = own_stat[...]
        for o, copy in enumerate(copies):
            copy.wait()
            total += got_stat[base + o]
        own_stat[...] = total
        base += count - 1
    stat_ref[...] = own_stat[...]


def solution(mesh):
    n, dpn = mesh.shape["fsdp"], mesh.shape["dp"]
    X = inner_of(n)
    Z = n // X
    q = n // dpn

    def local(data, start, noise, w1, w2, readout):
        R, K = start.shape
        H = w1.shape[1]
        C = H // n
        steps = noise.shape[0]
        S = 2 if R % 32 == 0 else 1
        h = R // S
        vmem = pl.BlockSpec(memory_space=pltpu.VMEM)
        dma = pltpu.SemaphoreType.DMA
        kinds = 2 + 2 * q
        peers = (X - 1) + (Z - 1) + (dpn - 1)
        raw1, raw2, stat = pl.pallas_call(
            functools.partial(kernel, n, X, dpn, steps, S),
            name="contrastive",
            out_shape=(
                jax.ShapeDtypeStruct((K, q * C), F32),
                jax.ShapeDtypeStruct((C, q * C), F32),
                jax.ShapeDtypeStruct((2, 8, 128), F32),
            ),
            in_specs=[vmem] * 6,
            out_specs=(vmem,) * 3,
            scratch_shapes=[
                pltpu.VMEM((R, K), F32),
                pltpu.VMEM((S, 2, Z, X - 1, h, C), BF16),
                pltpu.VMEM((S, 2, Z, X - 1, h, C), BF16),
                pltpu.VMEM((S, 2, Z - 1, h, C), BF16),
                pltpu.VMEM((S, 2, Z - 1, h, C), BF16),
                pltpu.VMEM((S, Z, h, C), F32),
                pltpu.VMEM((S, 2, n, h, C), BF16),
                pltpu.VMEM((S, 2, n, h, C), BF16),
                pltpu.VMEM((2, dpn, S, h, K), BF16),
                pltpu.VMEM((2, dpn, S, h, C), BF16),
                pltpu.VMEM((2, 2, q, dpn, S, h, C), BF16),
                pltpu.VMEM((2, 8, 128), F32),
                pltpu.VMEM((peers, 2, 8, 128), F32),
                dma((S, 2, Z, X - 1)), dma((S, 2, Z, X - 1)),
                dma((S, 2, Z - 1)), dma((S, 2, Z - 1)),
                dma((S, 2, Z - 1)), dma((S, 2, Z - 1)),
                dma((S, 2, Z, X - 1)), dma((S, 2, Z, X - 1)),
                dma((2, kinds, dpn - 1, S)), dma((2, kinds, dpn - 1, S)),
                dma((peers,)), dma((peers,)),
            ],
            compiler_params=pltpu.CompilerParams(
                collective_id=0, has_side_effects=True, vmem_limit_bytes=60 * 1024 * 1024
            ),
        )(data, start, noise, w1, w2, readout.reshape(1, C))
        sums = jnp.sum(stat, axis=(1, 2))
        energy_gap = sums[0] / (R * dpn * 80.0 * jnp.sqrt(jnp.float32(H)))
        scale = jnp.sqrt(sums[1] / (2.0 * (K * n) * H) + 1e-06)
        return raw1 / scale, raw2 / scale, energy_gap

    in_specs = (
        P("dp", "fsdp"),
        P("dp", "fsdp"),
        P(None, "dp", "fsdp"),
        P("fsdp", None),
        P("fsdp", None),
        P("fsdp"),
    )
    out_specs = (P("fsdp", "dp"), P("fsdp", "dp"), P())
    return jax.shard_map(local, mesh=mesh, in_specs=in_specs, out_specs=out_specs, check_vma=False)
```

time: 433 us -> 377 us (0.87)
  Pallas kernels: 423 us -> 367 us
    pallas_call x1, Pallas kernels: 423 us -> 367 us  [local(): pl.pallas_call(functools.partial(kernel, n, X, dpn, steps, S), name='cont...]
where the time goes in v2:
time: 377 us
  Pallas kernels  367 us (97%)
  other arithmetic  5.86 us (2%)
    pallas_call x1, Pallas kernels, local(): pl.pallas_call(functools.partial(kernel, n, X, dpn, steps, S), name='cont...  367 us

profile of v2, /device:TPU:0, one launch (start us, length us, event | category | flops | bytes accessed | tf_op | source)
XLA Modules:
  0.0 376.9 jit_solution(4593319012607745427)
XLA Ops:
  0.6 367.3 %contrastive.1 = (f32[512,1024]{1,0:T(8,128)}, f32[512,1024]{1,0:T(8,128)}, f32[2,8,128]{2,1,0:T(8,128)}) custom-call(bf16[128,512]{1,0:T(8,128)(2,1)} %data_ref.1, f32[128,512]{1,0:T(8,128)} %start_ref.1, f32[4,128,512]{2,1,0:T(8,128)} %noise_ref.1, bf16[512,4096]{1,0:T(8,128)(2,1)} %w1_ref.1, bf16[512,4096]{1,0:T(8,128)(2,1)} %w2_ref.1, f32[1,512]{1,0:T(1,128)} %bitcast.3), custom_call_target="tpu_custom_call" | custom-call | tf_op jit(solution)/shard_map/contrastive/pallas_call | solution.py:358
  368.0 0.8 reduce_sum.9
  368.8 0.6 fusion
  370.7 5.1 %broadcast_divide_fusion = (f32[512,1024]{1,0:T(8,128)}, f32[512,1024]{1,0:T(8,128)}) fusion(f32[512,1024]{1,0:T(8,128)} %get-tuple-element.8, f32[]{:T(128)} %bitcast.1, f32[512,1024]{1,0:T(8,128)} %get-tuple-element.6), kind=kLoop, calls=%fused_computation | loop fusion | flops 1048576 | bytes 8388612 | tf_op jit(solution)/shard_map/div | solution.py:396
